TPU v7x, 32 devices: a whole 2x2x4 slice. The times are simulated.
32 devices in a mesh: aa: 2 (over core), ba: 16 (over z, y, x).
Axes of the slice: x: 2, y: 2, z: 4, core: 2. Of those that a mesh axis runs over, the one named last changes fastest.
Arguments:
- queries: bfloat16 [2, 16, 192, 1024], P('aa', 'ba'), may hold values from -6 to 6
- key_rows: bfloat16 [2, 16, 192, 1024], P('aa', 'ba'), may hold values from -6 to 6
- value_rows: bfloat16 [2, 16, 192, 1024], P('aa', 'ba'), may hold values from -6 to 6
- out_proj: bfloat16 [2, 1024, 1024], P('aa', 'ba'), may hold values from -0.1875 to 0.1875
- scale_ids: int32 [16, 192], P('ba'), may hold values from 0 to 7, never falling along the last dimension, each value on 1 to 64 neighbouring positions
- residual_in: bfloat16 [16, 192, 1024], P('ba'), may hold values from -4 to 4
- cotangent: bfloat16 [16, 192, 1024], P('ba'), may hold values from -6 to 6
Outputs:
- residual_out: bfloat16 [2, 16, 192, 1024], P('aa', 'ba')
- grad_query: bfloat16 [2, 16, 192, 1024], P('aa', 'ba')
- grad_key: bfloat16 [2, 16, 192, 1024], P('aa', 'ba')
- grad_value: bfloat16 [2, 16, 192, 1024], P('aa', 'ba')
- grad_proj: float32 [2, 1024, 1024], P('aa', 'ba')
Inputs may be any that keep to these rules, and one draw needn't show every extreme that they name: `scale_ids`: for each image the scale ids never fall along the tokens; every scale from 0 to 7 is present, with 1 to 64 tokens.
All inputs are finite; a program needn't handle non-finite values.
Results may differ from a plain program's by a relative error of at most 0.0086.
Values may be sent and summed in bfloat16 or wider, within the bound.
No kernel may reach another device: no remote copies, remote signals or barrier semaphores. Data moves between devices by JAX's collectives and lax.ppermute only.
A program may use at most 64 MiB of HBM per device.

v0:
```python
import jax
import jax.numpy as jnp
from jax import lax
from jax.sharding import PartitionSpec as P

HD = 64


def passed_along(value, axis, by):
    devices = lax.axis_size(axis)
    pairs = [(i, i + by) for i in range(devices) if 0 <= i + by < devices]
    return lax.ppermute(value, axis, pairs)


def local(queries, key_rows, value_rows, out_proj, scale_ids, residual_in, cotangent):
    images = queries.shape[1]
    length = queries.shape[2]
    inner_width = queries.shape[3]
    head_count = inner_width // HD
    res_width = residual_in.shape[2]
    flat_rows = images * length
    score_scale = HD ** (-0.5)
    image_weight = 1.0 / (lax.axis_size("ba") * images)
    w_full = lax.all_gather(out_proj, "ba", axis=1, tiled=True)[0]
    visible = scale_ids[:, None, :] <= scale_ids[:, :, None]
    q_heads = queries[0].reshape(images, length, head_count, HD)
    k_heads = key_rows[0].reshape(images, length, head_count, HD)
    v_heads = value_rows[0].reshape(images, length, head_count, HD)
    scores = (
        jnp.einsum("bihd,bjhd->bhij", q_heads, k_heads, preferred_element_type=jnp.float32)
        * score_scale
    )
    scores = jnp.where(visible[:, None], scores, -jnp.inf)
    row_max = jnp.max(scores, axis=-1, keepdims=True)
    lifted = jnp.exp(scores - row_max)
    attn_probs = lifted / jnp.sum(lifted, axis=-1, keepdims=True)
    probs_low = attn_probs.astype(jnp.bfloat16)
    attended = jnp.einsum("bhij,bjhd->bihd", probs_low, v_heads, preferred_element_type=jnp.float32)
    attn_rows = attended.astype(jnp.bfloat16).reshape(flat_rows, inner_width)
    branch = jnp.dot(attn_rows, w_full, preferred_element_type=jnp.float32)

    def relay_step(hop_index, running):
        return branch + passed_along(running, "aa", 1)

    carried = lax.fori_loop(0, lax.axis_size("aa") - 1, relay_step, branch)
    residual_rows = residual_in.reshape(flat_rows, res_width).astype(jnp.float32) + carried
    residual_out = residual_rows.astype(jnp.bfloat16).reshape(images, length, res_width)
    cot_rows = cotangent.reshape(flat_rows, res_width)
    d_attn = lax.dot_general(
        cot_rows, w_full, (((1,), (1,)), ((), ())), preferred_element_type=jnp.float32
    ).astype(jnp.bfloat16)
    product = lax.dot_general(
        attn_rows, cot_rows, (((0,), (0,)), ((), ())), preferred_element_type=jnp.float32
    )
    grad_proj = lax.psum_scatter(product * image_weight, "ba", scatter_dimension=0, tiled=True)
    d_heads = d_attn.reshape(images, length, head_count, HD)
    grad_value = jnp.einsum(
        "bhij,bihd->bjhd", probs_low, d_heads, preferred_element_type=jnp.float32
    )
    d_probs = jnp.einsum("bihd,bjhd->bhij", d_heads, v_heads, preferred_element_type=jnp.float32)
    row_delta = jnp.sum(attn_probs * d_probs, axis=-1, keepdims=True)
    d_scores = (attn_probs * (d_probs - row_delta) * score_scale).astype(jnp.bfloat16)
    grad_query = jnp.einsum(
        "bhij,bjhd->bihd", d_scores, k_heads, preferred_element_type=jnp.float32
    )
    grad_key = jnp.einsum("bhij,bihd->bjhd", d_scores, q_heads, preferred_element_type=jnp.float32)
    return (
        residual_out[None],
        grad_query.reshape(images, length, inner_width).astype(jnp.bfloat16)[None],
        grad_key.reshape(images, length, inner_width).astype(jnp.bfloat16)[None],
        grad_value.reshape(images, length, inner_width).astype(jnp.bfloat16)[None],
        grad_proj[None],
    )


def solution(mesh):
    placed = (
        P("aa", "ba", None, None),
        P("aa", "ba", None, None),
        P("aa", "ba", None, None),
        P("aa", "ba", None),
        P("ba", None),
        P("ba", None, None),
        P("ba", None, None),
    )
    return jax.shard_map(
        local,
        mesh=mesh,
        in_specs=placed,
        out_specs=(
            P("aa", "ba", None, None),
            P("aa", "ba", None, None),
            P("aa", "ba", None, None),
            P("aa", "ba", None, None),
            P("aa", "ba", None),
        ),
        check_vma=False,
    )
```

profile of v0, /device:TPU:0, one launch (start us, length us, event | category | flops | bytes accessed | tf_op | source)
XLA Modules:
  0.0 177.7 jit_solution(12900894556805366626)
XLA Ops:
  7.2 0.0 copy-start
  7.2 0.0 all-gather.2.cloned.1.call-start
  7.2 0.7 all-gather.2.cloned.1.call-update
  7.9 0.0 reduce-scatter.2.cloned.1.call-start
  8.0 1.2 copy.27
  9.2 0.0 copy-start.4
  9.2 1.4 copy.28
  10.6 0.0 copy-start.2
  10.6 1.4 copy.29
  12.0 0.8 broadcast_compare_fusion
  12.8 2.9 %fusion.44 = (f32[16,192]{1,0:T(8,128)S(1)}, f32[16,192,192]{1,2,0:T(8,128)}) fusion(pred[192,192]{0,1:T(8,128)(4,1)S(1)} %broadcast_compare_fusion, bf16[192,16,64]{0,2,1:T(8,128)(2,1)S(1)} %bitcast.69, bf16[192,16,64]{0,2,1:T(8,128)(2,1)S(1)} %bitcast.67), kind=kOutput, calls=%fused_computation.41 | convolution fusion | flops 77856960 | bytes 3194880 | tf_op jit(solution)/shard_map/sub | solution.py:35
  15.8 0.0 copy-done.4
  15.8 2.3 %convolution_convert_fusion = bf16[16,192,64]{1,2,0:T(8,128)(2,1)S(1)} fusion(bf16[192,16,64]{0,2,1:T(8,128)(2,1)S(1)} %bitcast.63, f32[16,192,192]{1,2,0:T(8,128)} %get-tuple-element.25, f32[16,192]{1,0:T(8,128)S(1)} %get-tuple-element.24), kind=kOutput, calls=%fused_computation.23 | convolution fusion | flops 76873728 | bytes 3158016 | tf_op jit(solution)/shard_map/bhij,bjhd->bihd/dot_general | solution.py:38
  18.1 2.6 %convolution_multiply_fusion = f32[1024,1024]{1,0:T(8,128)} fusion(bf16[192,1024]{0,1:T(8,128)(2,1)S(1)} %bitcast.61, bf16[1,192,1024]{2,1,0:T(8,128)(2,1)S(1)} %copy-done), kind=kOutput, calls=%fused_computation.8 | convolution fusion | flops 403701760 | bytes 4980736 | tf_op jit(solution)/shard_map/dot_general | solution.py:52
  20.7 0.0 reduce-scatter.2.cloned.1.call-update
  20.8 53.1 %all-gather.2.cloned.1.call-done = bf16[1,1024,1024]{2,1,0:T(8,128)(2,1)} async-done(((bf16[1,64,1024]{2,1,0:T(8,128)(2,1)}), bf16[1,1024,1024]{2,1,0:T(8,128)(2,1)}) %all-gather.2.cloned.1.call-update) | async-done | bytes 2097168 | tf_op jit(solution)/shard_map/all_gather | solution.py:24
  73.9 2.3 %fusion.8 = f32[192,1024]{1,0:T(8,128)S(1)} fusion(bf16[192,1024]{0,1:T(8,128)(2,1)S(1)} %bitcast.62, bf16[1,1024,1024]{2,1,0:T(8,128)(2,1)} %all-gather.2.cloned.1.call-done), kind=kOutput, calls=%fused_computation.11 | convolution fusion | flops 402653184 | bytes 3276800 | tf_op jit(solution)/shard_map/dot_general | solution.py:40
  76.2 1.3 collective-permute-start
  77.6 0.0 copy-done.1
  77.6 0.9 fusion.27
  78.5 0.2 copy.31
  78.7 2.3 %fusion.45 = f32[16,192,192]{1,2,0:T(8,128)} fusion(bf16[192,16,64]{0,2,1:T(8,128)(2,1)S(1)} %bitcast.65, bf16[192,16,64]{0,2,1:T(8,128)(2,1)S(1)} %bitcast.64), kind=kOutput, calls=%fused_computation.42 | convolution fusion | flops 75497472 | bytes 3145728 | tf_op jit(solution)/shard_map/bihd,bjhd->bhij/dot_general | solution.py:60
  81.0 0.0 copy-done.5
  81.0 6.6 %fusion.24 = bf16[16,192,64]{1,2,0:T(8,128)(2,1)} fusion(bf16[192,16,64]{0,2,1:T(8,128)(2,1)S(1)} %bitcast.70, f32[16,192,192]{1,2,0:T(8,128)} %fusion.45, f32[16,192,192]{1,2,0:T(8,128)} %get-tuple-element.25, f32[16,192]{1,0:T(8,128)S(1)} %get-tuple-element.24), kind=kOutput, calls=%fused_computation.22 | convolution fusion | flops 79826112 | bytes 5517312 | tf_op jit(solution)/shard_map/bhij,bihd->bjhd/dot_general | solution.py:66
  87.7 2.0 %copy.36 = bf16[1,1,192,1024]{3,2,1,0:T(8,128)(2,1)} copy(bf16[1,1,192,1024]{2,3,1,0:T(8,128)(2,1)} %bitcast.73) | data formatting | bytes 786432
  89.6 5.8 %fusion.21 = bf16[16,192,64]{1,2,0:T(8,128)(2,1)S(1)} fusion(bf16[192,16,64]{0,2,1:T(8,128)(2,1)S(1)} %bitcast.68, f32[16,192,192]{1,2,0:T(8,128)} %fusion.45, f32[16,192,192]{1,2,0:T(8,128)} %get-tuple-element.25, f32[16,192]{1,0:T(8,128)S(1)} %get-tuple-element.24), kind=kOutput, calls=%fused_computation.21 | convolution fusion | flops 79826112 | bytes 5517312 | tf_op jit(solution)/shard_map/bhij,bjhd->bihd/dot_general | solution.py:63
  95.5 0.9 copy.35
  96.4 2.6 %convolution_convert_fusion.1 = bf16[16,64,192]{2,1,0:T(8,128)(2,1)S(1)} fusion(bf16[192,16,64]{0,2,1:T(8,128)(2,1)S(1)} %bitcast.66, f32[16,192,192]{1,2,0:T(8,128)} %get-tuple-element.25, f32[16,192]{1,0:T(8,128)S(1)} %get-tuple-element.24), kind=kOutput, calls=%fused_computation.24 | convolution fusion | flops 76873728 | bytes 3158016 | tf_op jit(solution)/shard_map/bhij,bihd->bjhd/dot_general | solution.py:57
  99.0 0.9 copy.37
  99.9 0.0 collective-permute-done
  99.9 0.9 fusion.33
  100.9 69.9 %reduce-scatter.2.cloned.1.call-done = f32[64,1024]{1,0:T(8,128)} async-done(((f32[1024,1024]{1,0:T(8,128)}), f32[64,1024]{1,0:T(8,128)}) %reduce-scatter.2.cloned.1.call-update) | async-done | bytes 262160 | tf_op jit(solution)/shard_map/reduce_scatter | solution.py:55
  (8 shorter events, 0.0 us)
Async XLA Ops:
  7.2 10.9 %copy-start = (bf16[1,192,1024]{2,1,0:T(8,128)(2,1)S(1)}, bf16[1,192,1024]{2,1,0:T(8,128)(2,1)}, u32[]{:S(2)}) copy-start(bf16[1,192,1024]{2,1,0:T(8,128)(2,1)} %param.13) | copy-start | bytes 1179652
  7.2 66.7 %all-gather.2.cloned.1.call-start = ((), (), s32[]{:S(2)}) async-start(), calls=%async_computation.1 | async-start | bytes 2228224 | tf_op jit(solution)/shard_map/all_gather | solution.py:24
  7.9 162.9 %reduce-scatter.2.cloned.1.call-start = ((), (), s32[]{:S(2)}) async-start(), calls=%async_computation.2 | async-start | bytes 4456448 | tf_op jit(solution)/shard_map/reduce_scatter | solution.py:55
  9.2 6.6 %copy-start.4 = (bf16[1,1,192,1024]{2,3,1,0:T(8,128)(2,1)}, bf16[1,1,192,1024]{2,3,1,0:T(8,128)(2,1)S(1)}, u32[]{:S(2)}) copy-start(bf16[1,1,192,1024]{2,3,1,0:T(8,128)(2,1)S(1)} %copy.27) | copy-start | bytes 1179652
  10.6 5.2 %copy-start.2 = (bf16[1,1,192,1024]{2,3,1,0:T(8,128)(2,1)}, bf16[1,1,192,1024]{2,3,1,0:T(8,128)(2,1)S(1)}, u32[]{:S(2)}) copy-start(bf16[1,1,192,1024]{2,3,1,0:T(8,128)(2,1)S(1)} %copy.28) | copy-start | bytes 1179652
  73.9 3.7 %copy-start.1 = (bf16[1,1024,1024]{2,1,0:T(8,128)(2,1)S(1)}, bf16[1,1024,1024]{2,1,0:T(8,128)(2,1)}, u32[]{:S(2)}) copy-start(bf16[1,1024,1024]{2,1,0:T(8,128)(2,1)} %all-gather.2.cloned.1.call-done) | copy-start | bytes 6291460
  76.2 23.7 %collective-permute-start = (f32[192,1024]{1,0:T(8,128)S(1)}, f32[192,1024]{1,0:T(8,128)S(1)}, u32[]{:S(2)}, u32[]{:S(2)}) collective-permute-start(f32[192,1024]{1,0:T(8,128)S(1)} %fusion.8), channel_id=1, source_target_pairs={{0,16},{1,17},{2,18},{3,19},{4,20},{5,21},{6,22},{7,23},{8,24},{9,... | collective-permute-start | bytes 2359304 | tf_op jit(solution)/shard_map/while/body/eval_jaxpr/ppermute | solution.py:12
  78.7 2.4 %copy-start.5 = (bf16[1,1,192,1024]{2,3,1,0:T(8,128)(2,1)S(1)}, bf16[1,1,192,1024]{2,3,1,0:T(8,128)(2,1)}, u32[]{:S(2)}) copy-start(bf16[1,1,192,1024]{2,3,1,0:T(8,128)(2,1)} %copy-done.4) | copy-start | bytes 1179652
  81.0 8.6 %copy-start.3 = (bf16[1,1,192,1024]{2,3,1,0:T(8,128)(2,1)S(1)}, bf16[1,1,192,1024]{2,3,1,0:T(8,128)(2,1)}, u32[]{:S(2)}) copy-start(bf16[1,1,192,1024]{2,3,1,0:T(8,128)(2,1)} %copy-done.2) | copy-start | bytes 1179652
  96.4 3.5 %copy-start.6 = (bf16[1,192,1024]{2,1,0:T(8,128)(2,1)S(1)}, bf16[1,192,1024]{2,1,0:T(8,128)(2,1)}, u32[]{:S(2)}) copy-start(bf16[1,192,1024]{2,1,0:T(8,128)(2,1)} %param.12) | copy-start | bytes 1179652
Sparse Core Ops, SparseCore 0:
  10.8 63.0 all-gather.1
  76.8 94.0 reduce-scatter.1
where the time goes:
time: 178 us
  waiting for transfers between devices  124 us (70%)
  matrix products  28.5 us (16%)
  between operations  14.2 us (8%)
  local copies, waits for them, and re-layouts  8.07 us (5%)
  other arithmetic  1.78 us (1%)
    reduce_scatter x1, waiting for transfers between devices, local(): lax.psum_scatter(product * image_weight, 'ba', scatter_dimension=0, tiled...  69.9 us
    all_gather x1, waiting for transfers between devices, local(): w_full = lax.all_gather(out_proj, 'ba', axis=1, tiled=True)[0]  53.1 us
    unnamed x20, local copies, waits for them, and re-layouts  7.87 us
    dot_general x1, matrix products, local(): jnp.einsum('bhij,bihd->bjhd', d_scores, q_heads, preferred_element_type=j...  6.62 us
    dot_general x1, matrix products, local(): jnp.einsum('bhij,bjhd->bihd', d_scores, k_heads, preferred_element_type=j...  5.82 us
  transfers between devices with their start and end apart: 3, of which 2 were waited for; matrix products, arithmetic and copies ran while one was open for 22% of the time, Pallas kernels for 0%

commit v1 on v0

--- a/solution.py
+++ b/solution.py
@@ -21,7 +21,7 @@
     flat_rows = images * length
     score_scale = HD ** (-0.5)
     image_weight = 1.0 / (lax.axis_size("ba") * images)
-    w_full = lax.all_gather(out_proj, "ba", axis=1, tiled=True)[0]
+    w_full = jnp.concatenate(lax.all_gather(out_proj, "ba"), axis=1)[0]
     visible = scale_ids[:, None, :] <= scale_ids[:, :, None]
     q_heads = queries[0].reshape(images, length, head_count, HD)
     k_heads = key_rows[0].reshape(images, length, head_count, HD)

time: 178 us -> 178 us (level)
  no operation moved by 1% of the time
where the time goes in v1:
time: 178 us
  waiting for transfers between devices  124 us (70%)
  matrix products  28.5 us (16%)
  between operations  14.2 us (8%)
  local copies, waits for them, and re-layouts  8.07 us (5%)
  other arithmetic  1.78 us (1%)
    reduce_scatter x1, waiting for transfers between devices, local(): lax.psum_scatter(product * image_weight, 'ba', scatter_dimension=0, tiled...  69.9 us
    all_gather x1, waiting for transfers between devices, local(): w_full = jnp.concatenate(lax.all_gather(out_proj, 'ba'), axis=1)[0]  53.1 us
    unnamed x20, local copies, waits for them, and re-layouts  7.87 us
    dot_general x1, matrix products, local(): jnp.einsum('bhij,bihd->bjhd', d_scores, q_heads, preferred_element_type=j...  6.62 us
    dot_general x1, matrix products, local(): jnp.einsum('bhij,bjhd->bihd', d_scores, k_heads, preferred_element_type=j...  5.82 us
  transfers between devices with their start and end apart: 3, of which 2 were waited for; matrix products, arithmetic and copies ran while one was open for 22% of the time, Pallas kernels for 0%

profile of v1, /device:TPU:0, one launch (start us, length us, event | category | flops | bytes accessed | tf_op | source)
XLA Modules:
  0.0 177.7 jit_solution(5062084728257037514)
XLA Ops:
  7.2 0.0 copy-start
  7.2 0.0 all-gather.3.cloned.1.call-start
  7.2 0.7 all-gather.3.cloned.1.call-update
  7.9 0.0 reduce-scatter.2.cloned.1.call-start
  8.0 1.2 copy.38
  9.2 0.0 copy-start.4
  9.2 1.4 copy.39
  10.6 0.0 copy-start.2
  10.6 1.4 copy.40
  12.0 0.8 broadcast_compare_fusion
  12.8 2.9 %fusion.37 = (f32[16,192]{1,0:T(8,128)S(1)}, f32[16,192,192]{1,2,0:T(8,128)}) fusion(pred[192,192]{0,1:T(8,128)(4,1)S(1)} %broadcast_compare_fusion, bf16[192,16,64]{0,2,1:T(8,128)(2,1)S(1)} %bitcast.67, bf16[192,16,64]{0,2,1:T(8,128)(2,1)S(1)} %bitcast.65), kind=kOutput, calls=%fused_computation.37 | convolution fusion | flops 77856960 | bytes 3194880 | tf_op jit(solution)/shard_map/sub | solution.py:35
  15.8 0.0 copy-done.4
  15.8 2.3 %convolution_convert_fusion = bf16[16,192,64]{1,2,0:T(8,128)(2,1)S(1)} fusion(bf16[192,16,64]{0,2,1:T(8,128)(2,1)S(1)} %bitcast.61, f32[16,192,192]{1,2,0:T(8,128)} %get-tuple-element.30, f32[16,192]{1,0:T(8,128)S(1)} %get-tuple-element.29), kind=kOutput, calls=%fused_computation.19 | convolution fusion | flops 76873728 | bytes 3158016 | tf_op jit(solution)/shard_map/bhij,bjhd->bihd/dot_general | solution.py:38
  18.1 2.6 %convolution_multiply_fusion = f32[1024,1024]{1,0:T(8,128)} fusion(bf16[192,1024]{0,1:T(8,128)(2,1)S(1)} %bitcast.59, bf16[1,192,1024]{2,1,0:T(8,128)(2,1)S(1)} %copy-done), kind=kOutput, calls=%fused_computation.8 | convolution fusion | flops 403701760 | bytes 4980736 | tf_op jit(solution)/shard_map/dot_general | solution.py:52
  20.7 0.0 reduce-scatter.2.cloned.1.call-update
  20.8 53.1 %all-gather.3.cloned.1.call-done = bf16[16,64,1024]{2,1,0:T(8,128)(2,1)} async-done(((bf16[1,64,1024]{2,1,0:T(8,128)(2,1)}), bf16[16,64,1024]{2,1,0:T(8,128)(2,1)}) %all-gather.3.cloned.1.call-update) | async-done | bytes 2097168 | tf_op jit(solution)/shard_map/all_gather | solution.py:24
  73.9 2.3 %fusion.38 = f32[192,1024]{1,0:T(8,128)S(1)} fusion(bf16[192,1024]{0,1:T(8,128)(2,1)S(1)} %bitcast.60, bf16[1024,1024]{1,0:T(8,128)(2,1)} %bitcast.57), kind=kOutput, calls=%fused_computation.38 | convolution fusion | flops 402653184 | bytes 3276800 | tf_op jit(solution)/shard_map/dot_general | solution.py:40
  76.2 1.3 collective-permute-start
  77.6 0.0 copy-done.1
  77.6 0.9 convolution_convert_fusion.2
  78.5 0.2 copy.42
  78.7 2.3 %fusion.39 = f32[16,192,192]{1,2,0:T(8,128)} fusion(bf16[192,16,64]{0,2,1:T(8,128)(2,1)S(1)} %bitcast.63, bf16[192,16,64]{0,2,1:T(8,128)(2,1)S(1)} %bitcast.62), kind=kOutput, calls=%fused_computation.39 | convolution fusion | flops 75497472 | bytes 3145728 | tf_op jit(solution)/shard_map/bihd,bjhd->bhij/dot_general | solution.py:60
  81.0 0.0 copy-done.5
  81.0 6.6 %fusion.20 = bf16[16,192,64]{1,2,0:T(8,128)(2,1)} fusion(bf16[192,16,64]{0,2,1:T(8,128)(2,1)S(1)} %bitcast.68, f32[16,192,192]{1,2,0:T(8,128)} %fusion.39, f32[16,192,192]{1,2,0:T(8,128)} %get-tuple-element.30, f32[16,192]{1,0:T(8,128)S(1)} %get-tuple-element.29), kind=kOutput, calls=%fused_computation.18 | convolution fusion | flops 79826112 | bytes 5517312 | tf_op jit(solution)/shard_map/bhij,bihd->bjhd/dot_general | solution.py:66
  87.7 2.0 %copy.47 = bf16[1,1,192,1024]{3,2,1,0:T(8,128)(2,1)} copy(bf16[1,1,192,1024]{2,3,1,0:T(8,128)(2,1)} %bitcast.71) | data formatting | bytes 786432
  89.6 5.8 %fusion.17 = bf16[16,192,64]{1,2,0:T(8,128)(2,1)S(1)} fusion(bf16[192,16,64]{0,2,1:T(8,128)(2,1)S(1)} %bitcast.66, f32[16,192,192]{1,2,0:T(8,128)} %fusion.39, f32[16,192,192]{1,2,0:T(8,128)} %get-tuple-element.30, f32[16,192]{1,0:T(8,128)S(1)} %get-tuple-element.29), kind=kOutput, calls=%fused_computation.17 | convolution fusion | flops 79826112 | bytes 5517312 | tf_op jit(solution)/shard_map/bhij,bjhd->bihd/dot_general | solution.py:63
  95.5 0.9 copy.46
  96.4 2.6 %convolution_convert_fusion.1 = bf16[16,64,192]{2,1,0:T(8,128)(2,1)S(1)} fusion(bf16[192,16,64]{0,2,1:T(8,128)(2,1)S(1)} %bitcast.64, f32[16,192,192]{1,2,0:T(8,128)} %get-tuple-element.30, f32[16,192]{1,0:T(8,128)S(1)} %get-tuple-element.29), kind=kOutput, calls=%fused_computation.20 | convolution fusion | flops 76873728 | bytes 3158016 | tf_op jit(solution)/shard_map/bhij,bihd->bjhd/dot_general | solution.py:57
  99.0 0.9 copy.48
  99.9 0.0 collective-permute-done
  99.9 0.9 fusion.26
  100.9 69.9 %reduce-scatter.2.cloned.1.call-done = f32[64,1024]{1,0:T(8,128)} async-done(((f32[1024,1024]{1,0:T(8,128)}), f32[64,1024]{1,0:T(8,128)}) %reduce-scatter.2.cloned.1.call-update) | async-done | bytes 262160 | tf_op jit(solution)/shard_map/reduce_scatter | solution.py:55
  (8 shorter events, 0.0 us)
Async XLA Ops:
  7.2 10.9 %copy-start = (bf16[1,192,1024]{2,1,0:T(8,128)(2,1)S(1)}, bf16[1,192,1024]{2,1,0:T(8,128)(2,1)}, u32[]{:S(2)}) copy-start(bf16[1,192,1024]{2,1,0:T(8,128)(2,1)} %param.13) | copy-start | bytes 1179652
  7.2 66.7 %all-gather.3.cloned.1.call-start = ((), (), s32[]{:S(2)}) async-start(), calls=%async_computation.2 | async-start | bytes 2228224 | tf_op jit(solution)/shard_map/all_gather | solution.py:24
  7.9 162.9 %reduce-scatter.2.cloned.1.call-start = ((), (), s32[]{:S(2)}) async-start(), calls=%async_computation.1 | async-start | bytes 4456448 | tf_op jit(solution)/shard_map/reduce_scatter | solution.py:55
  9.2 6.6 %copy-start.4 = (bf16[1,1,192,1024]{2,3,1,0:T(8,128)(2,1)}, bf16[1,1,192,1024]{2,3,1,0:T(8,128)(2,1)S(1)}, u32[]{:S(2)}) copy-start(bf16[1,1,192,1024]{2,3,1,0:T(8,128)(2,1)S(1)} %copy.38) | copy-start | bytes 1179652
  10.6 5.2 %copy-start.2 = (bf16[1,1,192,1024]{2,3,1,0:T(8,128)(2,1)}, bf16[1,1,192,1024]{2,3,1,0:T(8,128)(2,1)S(1)}, u32[]{:S(2)}) copy-start(bf16[1,1,192,1024]{2,3,1,0:T(8,128)(2,1)S(1)} %copy.39) | copy-start | bytes 1179652
  73.9 3.7 %copy-start.1 = (bf16[16,64,1024]{2,1,0:T(8,128)(2,1)S(1)}, bf16[16,64,1024]{2,1,0:T(8,128)(2,1)}, u32[]{:S(2)}) copy-start(bf16[16,64,1024]{2,1,0:T(8,128)(2,1)} %all-gather.3.cloned.1.call-done) | copy-start | bytes 6291460
  76.2 23.7 %collective-permute-start = (f32[192,1024]{1,0:T(8,128)S(1)}, f32[192,1024]{1,0:T(8,128)S(1)}, u32[]{:S(2)}, u32[]{:S(2)}) collective-permute-start(f32[192,1024]{1,0:T(8,128)S(1)} %fusion.38), channel_id=1, source_target_pairs={{0,16},{1,17},{2,18},{3,19},{4,20},{5,21},{6,22},{7,23},{8,24},{9,... | collective-permute-start | bytes 2359304 | tf_op jit(solution)/shard_map/while/body/eval_jaxpr/ppermute | solution.py:12
  78.7 2.4 %copy-start.5 = (bf16[1,1,192,1024]{2,3,1,0:T(8,128)(2,1)S(1)}, bf16[1,1,192,1024]{2,3,1,0:T(8,128)(2,1)}, u32[]{:S(2)}) copy-start(bf16[1,1,192,1024]{2,3,1,0:T(8,128)(2,1)} %copy-done.4) | copy-start | bytes 1179652
  81.0 8.6 %copy-start.3 = (bf16[1,1,192,1024]{2,3,1,0:T(8,128)(2,1)S(1)}, bf16[1,1,192,1024]{2,3,1,0:T(8,128)(2,1)}, u32[]{:S(2)}) copy-start(bf16[1,1,192,1024]{2,3,1,0:T(8,128)(2,1)} %copy-done.2) | copy-start | bytes 1179652
  96.4 3.5 %copy-start.6 = (bf16[1,192,1024]{2,1,0:T(8,128)(2,1)S(1)}, bf16[1,192,1024]{2,1,0:T(8,128)(2,1)}, u32[]{:S(2)}) copy-start(bf16[1,192,1024]{2,1,0:T(8,128)(2,1)} %param.12) | copy-start | bytes 1179652
Sparse Core Ops, SparseCore 0:
  10.8 63.0 all-gather.2
  76.8 94.0 reduce-scatter.1
